TPU v7x, 32 devices: a 4x4x1 block of a 4x4x8 slice. The times are simulated.
32 devices in a mesh: part: 1 (over z), dp: 32 (over y, x, core).
Axes of the slice: x: 4, y: 4, z: 1, core: 2. Of those that a mesh axis runs over, the one named last changes fastest.
The devices are a block of a 4x4x8 slice.
Arguments:
- tokens: bfloat16 [96, 384, 2048], P(('part', 'dp'))
- lengths: int32 [96], P(('part', 'dp'))
- ln1_gain: bfloat16 [2, 2048], P(None, 'dp')
- ln1_bias: bfloat16 [2, 2048], P(None, 'dp')
- w_attn: bfloat16 [2, 2048, 2304], P(None, 'dp')
- b_attn: bfloat16 [2, 2304], P(None, 'dp')
- w_out: bfloat16 [2, 2048, 2048], P(None, 'dp')
- b_out: bfloat16 [2, 2048], P(None, 'dp')
- ln2_gain: bfloat16 [2, 2048], P(None, 'dp')
- ln2_bias: bfloat16 [2, 2048], P(None, 'dp')
- w_fc: bfloat16 [2, 2048, 8192], P(None, 'dp')
- b_fc: bfloat16 [2, 8192], P(None, 'dp')
- w_proj: bfloat16 [2, 8192, 2048], P(None, 'dp')
- b_proj: bfloat16 [2, 2048], P(None, 'dp')
Outputs:
- output 1: bfloat16 [96, 384, 2048], P(('part', 'dp'))
- output 2: bfloat16 [96, 2, 384, 128], P(('part', 'dp'))
- output 3: bfloat16 [96, 2, 384, 128], P(('part', 'dp'))
All inputs are finite; a program needn't handle non-finite values.
Results may differ from a plain program's by a relative error of at most 0.0192267.
Values are sent between devices in bfloat16 or wider.
A program may use at most 768 MiB of HBM per device.

v0:
```python
import jax
import jax.numpy as jnp
from jax import lax
from jax.sharding import PartitionSpec as P

EPS = 1e-5


def layer_norm(values, gain, shift):
    wide = values.astype(jnp.float32)
    mean = jnp.mean(wide, axis=-1, keepdims=True)
    centred = wide - mean
    variance = jnp.mean(centred * centred, axis=-1, keepdims=True)
    normed = centred * lax.rsqrt(variance + EPS)
    return (normed * gain.astype(jnp.float32) + shift.astype(jnp.float32)).astype(jnp.bfloat16)


def dense(activation, weight, bias):
    return jnp.einsum('bsd,de->bse', activation, weight, preferred_element_type=jnp.float32) + bias.astype(jnp.float32)


def attention(query, keys, values, lengths):
    batch, seq_len, width = query.shape
    head = keys.shape[-1]
    q_heads = query.reshape(batch, seq_len, width // head, head)
    scores = jnp.einsum('bshd,btd->bsht', q_heads, keys, preferred_element_type=jnp.float32) * (head ** -0.5)
    position = jnp.arange(seq_len)
    allowed = (position[None, None, :] <= position[None, :, None]) & (position[None, None, :] < lengths[:, None, None])
    scores = jnp.where(allowed[:, :, None, :], scores, -1e30)
    attn_prob = jax.nn.softmax(scores, axis=-1).astype(jnp.bfloat16)
    mixed = jnp.einsum('bsht,btd->bshd', attn_prob, values, preferred_element_type=jnp.float32)
    return mixed.astype(jnp.bfloat16).reshape(batch, seq_len, width)


def layer_forward(state, lengths, params):
    ln1_gain, ln1_bias, w_attn, b_attn, w_out, b_out, ln2_gain, ln2_bias, w_fc, b_fc, w_proj, b_proj = params
    width = state.shape[-1]
    head = (w_attn.shape[-1] - width) // 2
    hidden = layer_norm(state, ln1_gain, ln1_bias)
    qkv_all = dense(hidden, w_attn, b_attn).astype(jnp.bfloat16)
    keys = qkv_all[..., width:width + head]
    values = qkv_all[..., width + head:]
    attended = attention(qkv_all[..., :width], keys, values, lengths)
    residual = (state.astype(jnp.float32) + dense(attended, w_out, b_out)).astype(jnp.bfloat16)
    hidden2 = layer_norm(residual, ln2_gain, ln2_bias)
    inner = jax.nn.gelu(dense(hidden2, w_fc, b_fc), approximate=True).astype(jnp.bfloat16)
    updated = (residual.astype(jnp.float32) + dense(inner, w_proj, b_proj)).astype(jnp.bfloat16)
    return updated, keys, values


def solution(mesh):
    tok_spec = P(('part', 'dp'), None, None)
    len_spec = P(('part', 'dp'))
    cache_spec = P(('part', 'dp'), None, None, None)
    vec_spec = P(None, 'dp')
    mat_spec = P(None, 'dp', None)

    def local(tokens, lengths, ln1_gain, ln1_bias, w_attn, b_attn, w_out, b_out, ln2_gain, ln2_bias, w_fc, b_fc, w_proj, b_proj):
        stacked = (ln1_gain, ln1_bias, w_attn, b_attn, w_out, b_out, ln2_gain, ln2_bias, w_fc, b_fc, w_proj, b_proj)
        state = tokens
        key_list = []
        value_list = []
        for layer in range(ln1_gain.shape[0]):
            params = tuple(lax.all_gather(weight_stack[layer], 'dp', axis=0, tiled=True) for weight_stack in stacked)
            state, keys, values = layer_forward(state, lengths, params)
            key_list.append(keys)
            value_list.append(values)
        return state, jnp.stack(key_list, axis=1), jnp.stack(value_list, axis=1)

    return jax.shard_map(local, mesh=mesh,
                         in_specs=(tok_spec, len_spec, vec_spec, vec_spec, mat_spec, vec_spec, mat_spec, vec_spec, vec_spec, vec_spec, mat_spec, vec_spec, mat_spec, vec_spec),
                         out_specs=(tok_spec, cache_spec, cache_spec), check_vma=False)
```

profile of v0, /device:TPU:97, one launch (start us, length us, event | category | flops | bytes accessed | tf_op | source)
XLA Modules:
  0.0 711.7 jit_solution(14280849299456839428)
XLA Ops:
  7.4 2.0 fusion.174
  9.5 1.9 fusion.175
  11.5 3.1 fusion.172
  14.7 1.5 fusion.173
  17.6 0.7 all-gather.45.cloned.1.call-update
  18.5 0.7 all-gather.47.cloned.1.call-update
  19.8 1.4 dynamic-update-slice
  21.8 1.4 dynamic-update-slice.1
  23.9 1.4 dynamic-update-slice.10
  25.2 0.6 broadcast.147.clone.11
  25.8 1.4 dynamic-update-slice.11
  27.8 1.4 dynamic-update-slice.12
  29.8 1.4 dynamic-update-slice.13
  33.0 51.4 %all-reduce.14 = (bf16[2048]{0:T(1024)(128)(2,1)S(1)}, bf16[2304]{0:T(1024)(128)(2,1)S(1)}, bf16[2048]{0:T(1024)(128)(2,1)S(1)}, bf16[2048]{0:T(1024)(128)(2,1)S...) all-reduce(bf16[2048]{0:T(1024)(128)(2,1)S(1)} %dynamic-update-slic, ...), channel_id=7, replica_groups=mesh['part'=1,'dp'=32] {'dp'}, use_global_device_ids=true, to_apply=%add.3 | all-reduce | flops 29184 | bytes 116736
  84.5 27.2 %all-gather.9 = bf16[1,8192]{1,0:T(2,128)(2,1)S(1)} all-gather(bf16[1,256]{1,0:T(2,128)(2,1)S(1)} %get-tuple-element.33), channel_id=11, replica_groups=mesh['part'=1,'dp'=32] {'dp'}, dimensions={1}, use_global_device_ids=true | all-gather | bytes 16896 | tf_op jit(solution)/shard_map/all_gather | solution.py:64
  112.3 0.6 convert_element_type.173
  115.3 0.6 convert_element_type.176
  115.9 32.0 %all-gather.21 = bf16[1,8192]{1,0:T(2,128)(2,1)S(1)} all-gather(bf16[1,256]{1,0:T(2,128)(2,1)S(1)} %get-tuple-element.32), channel_id=23, replica_groups=mesh['part'=1,'dp'=32] {'dp'}, dimensions={1}, use_global_device_ids=true | all-gather | bytes 16896 | tf_op jit(solution)/shard_map/all_gather | solution.py:64
  147.9 0.6 convert_element_type.162
  149.3 3.0 convert_reduce_fusion.3
  152.3 3.7 fusion.74
  156.3 17.0 %add_convert_fusion.1 = bf16[3,384,2304]{2,1,0:T(8,128)(2,1)S(1)} fusion(bf16[1,2048,2304]{2,1,0:T(8,128)(2,1)} %all-gather.33.cloned.1.call-done, f32[2304]{0:T(1024)S(1)} %convert_element_type.166, bf16[3,384,2048]{2,1,0:T(8,128)(2,1)} %param.14, f32[2048]{0:T(1024)S(1)} %convert_element_type.165, f32[2048]{0:T(1024)S(1)} %convert_element_type.164, ...), kind=kOutput, calls=%fused_computation.73 | convolution fusion | flops 10891100160 | bytes 19499008 | tf_op jit(solution)/shard_map/bsd,de->bse/dot_general | solution.py:19
  173.3 2.3 copy-done
  175.7 11.2 %fusion.103 = f32[3,384,16,384]{1,3,2,0:T(8,128)} fusion(bf16[3,384,2304]{2,1,0:T(8,128)(2,1)S(1)} %add_convert_fusion.1), kind=kOutput, calls=%fused_computation.105 | convolution fusion | flops 1811939328 | bytes 33325056 | tf_op jit(solution)/shard_map/bshd,btd->bsht/dot_general | solution.py:26
  186.9 32.0 %fusion.177 = (f32[3,384,16]{1,2,0:T(8,128)S(1)}, f32[3,384,16,384]{1,3,2,0:T(8,128)}) fusion(f32[3,384,16,384]{1,3,2,0:T(8,128)} %fusion.103, pred[3,384,384]{1,2,0:T(8,128)(4,1)S(1)} %broadcast_and_fusion), kind=kOutput, calls=%fused_computation.184 | output fusion | flops 42467712 | bytes 57139200 | tf_op jit(solution)/shard_map/sub | solution.py:30
  218.9 13.1 %fusion.151 = bf16[3,384,16,128]{1,3,2,0:T(8,128)(2,1)} fusion(f32[3,384,16,384]{1,3,2,0:T(8,128)} %get-tuple-element.49, f32[3,384,16]{1,2,0:T(8,128)S(1)} %get-tuple-element.48, bf16[3,384,2304]{2,1,0:T(8,128)(2,1)} %copy-done), kind=kOutput, calls=%fused_computation.127 | convolution fusion | flops 1828454400 | bytes 33398784 | tf_op jit(solution)/shard_map/bsht,btd->bshd/dot_general | solution.py:31
  232.0 15.6 %convert_reduce_fusion.2 = (f32[3,384]{1,0:T(4,128)S(1)}, bf16[3,384,2048]{2,1,0:T(8,128)(2,1)S(1)}) fusion(f32[2048]{0:T(1024)S(1)} %convert_element_type.167, bf16[3,384,2048]{1,2,0:T(8,128)(2,1)} %bitcast.153, bf16[1,2048,2048]{2,1,0:T(8,128)(2,1)} %all-gather.35.cloned.1.call-done, bf16[3,384,2048]{2,1,0:T(8,128)(2,1)} %param.14), kind=kOutput, calls=%fused_computation.60 | convolution fusion | flops 9677831168 | bytes 22557184 | tf_op jit(solution)/shard_map/bsd,de->bse/dot_general | solution.py:19
  247.7 2.2 copy-done.3
  249.8 1.4 fusion.70
  251.2 1.9 slice_bitcast_fusion.4
  253.1 55.1 %fusion.141.clone.4 = bf16[3,384,8192]{2,1,0:T(8,128)(2,1)} fusion(f32[8192]{0:T(1024)S(1)} %bitcast.151, bf16[1,2048,8192]{2,1,0:T(8,128)(2,1)} %all-gather.37.cloned.1.call-done, bf16[3,384,2048]{2,1,0:T(8,128)(2,1)} %copy-done.3, f32[2048]{0:T(1024)S(1)} %convert_element_type.169, ...), kind=kOutput, calls=%fused_computation.11.clone.clone.clone.clone.clone.clone.1 | convolution fusion | flops 38763233280 | bytes 57205760 | tf_op jit(solution)/shard_map/bsd,de->bse/dot_general | solution.py:19
  308.2 25.8 %all-gather.39.cloned.1.call-done = bf16[1,8192,2048]{2,1,0:T(8,128)(2,1)} async-done(((bf16[1,256,2048]{2,1,0:T(8,128)(2,1)}), bf16[1,8192,2048]{2,1,0:T(8,128)(2,1)}) %all-gather.39.cloned.1.call-update) | async-done | bytes 33554448 | tf_op jit(solution)/shard_map/all_gather | solution.py:64
  334.1 49.9 %convert_reduce_fusion.1 = (f32[3,384]{1,0:T(4,128)S(1)}, bf16[3,384,2048]{2,1,0:T(8,128)(2,1)S(1)}) fusion(f32[2048]{0:T(1024)S(1)} %copy-done.18, bf16[1,8192,2048]{2,1,0:T(8,128)(2,1)} %all-gather.39.cloned.1.call-done, bf16[3,384,2048]{2,1,0:T(8,128)(2,1)} %copy-done.3, bf16[3,384,8192]{2,1,0:T(8,128)(2,1)} %fusion.141.clone.4), kind=kOutput, calls=%fused_computation.57 | convolution fusion | flops 38668861440 | bytes 61878784 | tf_op jit(solution)/shard_map/bsd,de->bse/dot_general | solution.py:19
  384.0 2.2 copy-done.2
  386.1 1.4 fusion.66
  387.6 16.8 %add_convert_fusion = bf16[3,384,2304]{2,1,0:T(8,128)(2,1)S(1)} fusion(bf16[1,2048,2304]{2,1,0:T(8,128)(2,1)} %all-gather.41.cloned.1.call-done, f32[2304]{0:T(1024)S(1)} %copy-done.11, bf16[3,384,2048]{2,1,0:T(8,128)(2,1)} %copy-done.2, f32[2048]{0:T(1024)S(1)} %copy-done.17, f32[2048]{0:T(1024)S(1)} %copy-done.16, f32[3,384]{1,0:T(4,128)S(1)} %add_rsqrt_fusion.1, ...), kind=kOutput, calls=%fused_computation.72 | convolution fusion | flops 10891100160 | bytes 19499008 | tf_op jit(solution)/shard_map/bsd,de->bse/dot_general | solution.py:19
  404.7 1.0 copy.25
  405.7 1.4 copy.26
  407.2 11.3 %fusion.100 = f32[3,384,16,384]{1,3,2,0:T(8,128)} fusion(bf16[3,384,2304]{2,1,0:T(8,128)(2,1)S(1)} %add_convert_fusion), kind=kOutput, calls=%fused_computation.102 | convolution fusion | flops 1811939328 | bytes 33325056 | tf_op jit(solution)/shard_map/bshd,btd->bsht/dot_general | solution.py:26
  418.5 32.2 %fusion.182 = (f32[3,384,16]{1,2,0:T(8,128)S(1)}, f32[3,384,16,384]{1,3,2,0:T(8,128)}) fusion(f32[3,384,16,384]{1,3,2,0:T(8,128)} %fusion.100, pred[3,384,384]{1,2,0:T(8,128)(4,1)S(1)} %copy-done.9), kind=kOutput, calls=%fused_computation.185 | output fusion | flops 42467712 | bytes 57139200 | tf_op jit(solution)/shard_map/sub | solution.py:30
  450.7 13.1 %fusion.150 = bf16[3,384,16,128]{1,3,2,0:T(8,128)(2,1)} fusion(f32[3,384,16,384]{1,3,2,0:T(8,128)} %get-tuple-element.55, f32[3,384,16]{1,2,0:T(8,128)S(1)} %get-tuple-element.54, bf16[3,384,2304]{2,1,0:T(8,128)(2,1)} %copy-done.1), kind=kOutput, calls=%fused_computation.126 | convolution fusion | flops 1828454400 | bytes 33398784 | tf_op jit(solution)/shard_map/bsht,btd->bshd/dot_general | solution.py:31
  463.9 15.6 %convert_reduce_fusion = (f32[3,384]{1,0:T(4,128)S(1)}, bf16[3,384,2048]{2,1,0:T(8,128)(2,1)S(1)}) fusion(f32[2048]{0:T(1024)S(1)} %copy-done.15, bf16[3,384,2048]{1,2,0:T(8,128)(2,1)} %bitcast.152, bf16[1,2048,2048]{2,1,0:T(8,128)(2,1)} %all-gather.43.cloned.1.call-done, bf16[3,384,2048]{2,1,0:T(8,128)(2,1)} %copy-done.2), kind=kOutput, calls=%fused_computation.54 | convolution fusion | flops 9677831168 | bytes 22557184 | tf_op jit(solution)/shard_map/bsd,de->bse/dot_general | solution.py:19
  479.5 2.2 copy-done.4
  481.7 1.4 fusion.62
  483.0 61.3 %all-gather.45.cloned.1.call-done = bf16[1,2048,8192]{2,1,0:T(8,128)(2,1)} async-done(((bf16[1,64,8192]{2,1,0:T(8,128)(2,1)}), bf16[1,2048,8192]{2,1,0:T(8,128)(2,1)}) %all-gather.45.cloned.1.call-update) | async-done | bytes 33554448 | tf_op jit(solution)/shard_map/all_gather | solution.py:64
  544.4 54.7 %fusion.201 = bf16[3,384,8192]{2,1,0:T(8,128)(2,1)} fusion(f32[8192]{0:T(1024)S(1)} %bitcast.150, bf16[1,2048,8192]{2,1,0:T(8,128)(2,1)} %all-gather.45.cloned.1.call-done, bf16[3,384,2048]{2,1,0:T(8,128)(2,1)} %copy-done.4, f32[2048]{0:T(1024)S(1)} %copy-done.14, f32[2048]{0:T(1024)S(1)} %copy-done.13, ...), kind=kOutput, calls=%fused_computation.19.clone.clone.clone.clone.1 | convolution fusion | flops 38763233280 | bytes 57205760 | tf_op jit(solution)/shard_map/bsd,de->bse/dot_general | solution.py:19
  599.0 54.9 %all-gather.47.cloned.1.call-done = bf16[1,8192,2048]{2,1,0:T(8,128)(2,1)} async-done(((bf16[1,256,2048]{2,1,0:T(8,128)(2,1)}), bf16[1,8192,2048]{2,1,0:T(8,128)(2,1)}) %all-gather.47.cloned.1.call-update) | async-done | bytes 33554448 | tf_op jit(solution)/shard_map/all_gather | solution.py:64
  653.9 50.5 %fusion.81 = bf16[3,384,2048]{2,1,0:T(8,128)(2,1)} fusion(bf16[3,384,2048]{2,1,0:T(8,128)(2,1)} %copy-done.4, f32[2048]{0:T(1024)S(1)} %copy-done.12, bf16[1,8192,2048]{2,1,0:T(8,128)(2,1)} %all-gather.47.cloned.1.call-done, bf16[3,384,8192]{2,1,0:T(8,128)(2,1)} %fusion.201), kind=kOutput, calls=%fused_computation.93 | convolution fusion | flops 38664142848 | bytes 61874176 | tf_op jit(solution)/shard_map/bsd,de->bse/dot_general | solution.py:19
  (126 shorter events, 11.1 us)
Async XLA Ops:
  7.2 7.5 %copy-start.5 = (bf16[2,256,2048]{2,1,0:T(8,128)(2,1)S(1)}, bf16[2,256,2048]{2,1,0:T(8,128)(2,1)}, u32[]{:S(2)}) copy-start(bf16[2,256,2048]{2,1,0:T(8,128)(2,1)} %param.26) | copy-start | bytes 6291460
  7.2 12.0 %copy-start.20 = (bf16[2,64]{1,0:T(2,128)(2,1)S(1)}, bf16[2,64]{1,0:T(2,128)(2,1)}, u32[]{:S(2)}) copy-start(bf16[2,64]{1,0:T(2,128)(2,1)} %param.16) | copy-start | bytes 772
  7.2 14.0 %copy-start.21 = (bf16[2,64]{1,0:T(2,128)(2,1)S(1)}, bf16[2,64]{1,0:T(2,128)(2,1)}, u32[]{:S(2)}) copy-start(bf16[2,64]{1,0:T(2,128)(2,1)} %param.17) | copy-start | bytes 772
  7.2 16.0 %copy-start.22 = (bf16[2,64]{1,0:T(2,128)(2,1)S(1)}, bf16[2,64]{1,0:T(2,128)(2,1)}, u32[]{:S(2)}) copy-start(bf16[2,64]{1,0:T(2,128)(2,1)} %param.21) | copy-start | bytes 772
  7.2 18.0 %copy-start.23 = (bf16[2,64]{1,0:T(2,128)(2,1)S(1)}, bf16[2,64]{1,0:T(2,128)(2,1)}, u32[]{:S(2)}) copy-start(bf16[2,64]{1,0:T(2,128)(2,1)} %param.22) | copy-start | bytes 772
  7.2 20.0 %copy-start.24 = (bf16[2,64]{1,0:T(2,128)(2,1)S(1)}, bf16[2,64]{1,0:T(2,128)(2,1)}, u32[]{:S(2)}) copy-start(bf16[2,64]{1,0:T(2,128)(2,1)} %param.23) | copy-start | bytes 772
  7.2 22.0 %copy-start.25 = (bf16[2,64]{1,0:T(2,128)(2,1)S(1)}, bf16[2,64]{1,0:T(2,128)(2,1)}, u32[]{:S(2)}) copy-start(bf16[2,64]{1,0:T(2,128)(2,1)} %param.27) | copy-start | bytes 772
  7.3 25.3 %copy-start.26 = (bf16[2,72]{1,0:T(2,128)(2,1)S(1)}, bf16[2,72]{1,0:T(2,128)(2,1)}, u32[]{:S(2)}) copy-start(bf16[2,72]{1,0:T(2,128)(2,1)} %param.19) | copy-start | bytes 868
  7.3 77.2 %copy-start.19 = (bf16[2,256]{1,0:T(2,128)(2,1)S(1)}, bf16[2,256]{1,0:T(2,128)(2,1)}, u32[]{:S(2)}) copy-start(bf16[2,256]{1,0:T(2,128)(2,1)} %param.25) | copy-start | bytes 3076
  7.3 141.9 %copy-start.27 = (s32[3]{0:T(128)S(1)}, s32[3]{0:T(128)}, u32[]{:S(2)}) copy-start(s32[3]{0:T(128)} %param.15) | copy-start | bytes 40
  7.3 149.1 %all-gather.33.cloned.1.call-start = ((), (), s32[]{:S(2)}) async-start(), calls=%async_computation | async-start | bytes 9732096 | tf_op jit(solution)/shard_map/all_gather | solution.py:64
  9.4 222.6 %all-gather.35.cloned.1.call-start = ((), (), s32[]{:S(2)}) async-start(), calls=%async_computation.1 | async-start | bytes 8650752 | tf_op jit(solution)/shard_map/all_gather | solution.py:64
  11.4 241.7 %all-gather.37.cloned.1.call-start = ((), (), s32[]{:S(2)}) async-start(), calls=%async_computation.2 | async-start | bytes 34603008 | tf_op jit(solution)/shard_map/all_gather | solution.py:64
  14.7 319.4 %all-gather.39.cloned.1.call-start = ((), (), s32[]{:S(2)}) async-start(), calls=%async_computation.3 | async-start | bytes 34603008 | tf_op jit(solution)/shard_map/all_gather | solution.py:64
  16.3 371.3 %all-gather.41.cloned.1.call-start = ((), (), s32[]{:S(2)}) async-start(), calls=%async_computation.4 | async-start | bytes 9732096 | tf_op jit(solution)/shard_map/all_gather | solution.py:64
  16.9 446.9 %all-gather.43.cloned.1.call-start = ((), (), s32[]{:S(2)}) async-start(), calls=%async_computation.5 | async-start | bytes 8650752 | tf_op jit(solution)/shard_map/all_gather | solution.py:64
  17.6 526.8 %all-gather.45.cloned.1.call-start = ((), (), s32[]{:S(2)}) async-start(), calls=%async_computation.6 | async-start | bytes 34603008 | tf_op jit(solution)/shard_map/all_gather | solution.py:64
  18.4 635.5 %all-gather.47.cloned.1.call-start = ((), (), s32[]{:S(2)}) async-start(), calls=%async_computation.7 | async-start | bytes 34603008 | tf_op jit(solution)/shard_map/all_gather | solution.py:64
  156.3 30.6 %copy-start.8 = (pred[3,384,384]{1,2,0:T(8,128)(4,1)}, pred[3,384,384]{1,2,0:T(8,128)(4,1)S(1)}, u32[]{:S(2)}) copy-start(pred[3,384,384]{1,2,0:T(8,128)(4,1)S(1)} %broadcast_and_fusion) | copy-start | bytes 1327108
  173.3 2.3 copy-start
  247.6 2.2 copy-start.3
  253.1 80.9 %copy-start.18 = (f32[2048]{0:T(1024)S(1)}, f32[2048]{0:T(1024)}, u32[]{:S(2)}) copy-start(f32[2048]{0:T(1024)} %convert_element_type.170) | copy-start | bytes 24580
  308.2 79.4 %copy-start.11 = (f32[2304]{0:T(1024)S(1)}, f32[2304]{0:T(1024)}, u32[]{:S(2)}) copy-start(f32[2304]{0:T(1024)} %convert_element_type.173) | copy-start | bytes 27652
  308.2 79.4 %copy-start.16 = (f32[2048]{0:T(1024)S(1)}, f32[2048]{0:T(1024)}, u32[]{:S(2)}) copy-start(f32[2048]{0:T(1024)} %convert_element_type.171) | copy-start | bytes 24580
  308.2 79.4 %copy-start.17 = (f32[2048]{0:T(1024)S(1)}, f32[2048]{0:T(1024)}, u32[]{:S(2)}) copy-start(f32[2048]{0:T(1024)} %convert_element_type.172) | copy-start | bytes 24580
  383.9 2.2 copy-start.2
  387.5 17.1 %copy-start.6 = (bf16[3,1,384,128]{3,2,0,1:T(8,128)(2,1)S(1)}, bf16[3,1,384,128]{3,2,0,1:T(8,128)(2,1)}, u32[]{:S(2)}) copy-start(bf16[3,1,384,128]{3,2,0,1:T(8,128)(2,1)} %get-tuple-element.20) | copy-start | bytes 884740
  387.5 17.0 %copy-start.7 = (bf16[3,1,384,128]{3,2,0,1:T(8,128)(2,1)S(1)}, bf16[3,1,384,128]{3,2,0,1:T(8,128)(2,1)}, u32[]{:S(2)}) copy-start(bf16[3,1,384,128]{3,2,0,1:T(8,128)(2,1)} %get-tuple-element.21) | copy-start | bytes 884740
  404.4 2.7 copy-start.1
  407.2 11.3 %copy-start.9 = (pred[3,384,384]{1,2,0:T(8,128)(4,1)S(1)}, pred[3,384,384]{1,2,0:T(8,128)(4,1)}, u32[]{:S(2)}) copy-start(pred[3,384,384]{1,2,0:T(8,128)(4,1)} %copy-done.8) | copy-start | bytes 1327108
  450.7 13.1 %copy-start.15 = (f32[2048]{0:T(1024)S(1)}, f32[2048]{0:T(1024)}, u32[]{:S(2)}) copy-start(f32[2048]{0:T(1024)} %convert_element_type.174) | copy-start | bytes 24580
  463.8 80.5 %copy-start.10 = (f32[1,8192]{1,0:T(1,128)S(1)}, f32[1,8192]{1,0:T(1,128)}, u32[]{:S(2)}) copy-start(f32[1,8192]{1,0:T(1,128)} %convert_element_type.162) | copy-start | bytes 98308
  463.8 80.5 %copy-start.13 = (f32[2048]{0:T(1024)S(1)}, f32[2048]{0:T(1024)}, u32[]{:S(2)}) copy-start(f32[2048]{0:T(1024)} %convert_element_type.175) | copy-start | bytes 24580
  463.8 80.5 %copy-start.14 = (f32[2048]{0:T(1024)S(1)}, f32[2048]{0:T(1024)}, u32[]{:S(2)}) copy-start(f32[2048]{0:T(1024)} %convert_element_type.176) | copy-start | bytes 24580
  479.5 2.2 copy-start.4
  544.3 109.6 %copy-start.12 = (f32[2048]{0:T(1024)S(1)}, f32[2048]{0:T(1024)}, u32[]{:S(2)}) copy-start(f32[2048]{0:T(1024)} %convert_element_type.177) | copy-start | bytes 24580
Sparse Core Ops, SparseCore 0:
  10.8 54.9 all-gather.32
  67.9 46.7 all-gather.34
  116.7 107.8 all-gather.36
  226.6 107.4 all-gather.38
  336.6 49.0 all-gather.40
  387.6 46.8 all-gather.42
  436.6 107.7 all-gather.44
  546.4 107.4 all-gather.46
where the time goes:
time: 720 us; the launch traced here: 712 us
  matrix products  324 us (45%)
  waiting for transfers between devices  145 us (20%)
  blocking collectives  111 us (15%)
  other arithmetic  81.1 us (11%)
  local copies, waits for them, and re-layouts  35.6 us (5%)
  between operations  15.1 us (2%)
    dot_general x8, matrix products, dense(): jnp.einsum('bsd,de->bse', activation, weight, preferred_element_type=jnp....  275 us
    all_gather x8, waiting for transfers between devices, local(): lax.all_gather(weight_stack[layer], 'dp', axis=0, tiled=True)  142 us
    sub x2, other arithmetic, attention(): attn_prob = jax.nn.softmax(scores, axis=-1).astype(jnp.bfloat16)  64.3 us
    all_gather x2, blocking collectives, local(): lax.all_gather(weight_stack[layer], 'dp', axis=0, tiled=True)  59.2 us
    unnamed x1, blocking collectives  51.4 us
    dot_general x2, matrix products, attention(): jnp.einsum('bsht,btd->bshd', attn_prob, values, preferred_element_type=jn...  26.2 us
    unnamed x93, local copies, waits for them, and re-layouts  25.2 us
    dot_general x2, matrix products, attention(): jnp.einsum('bshd,btd->bsht', q_heads, keys, preferred_element_type=jnp.fl...  22.6 us
  transfers between devices with their start and end apart: 8, of which 3 were waited for; matrix products, arithmetic and copies ran while one was open for 53% of the time, Pallas kernels for 0%

commit v1 on v0

v1 whole, which is shorter than its diff:
```python
import functools
import math

import jax
import jax.numpy as jnp
from jax import lax
from jax.experimental import pallas as pl
from jax.experimental.pallas import tpu as pltpu
from jax.sharding import PartitionSpec as P

EPS = 1e-5
F32 = jnp.float32
BF16 = jnp.bfloat16
FC_PARTS = 4
PROJ_PARTS = 4
VROWS = 16
VCOLS = 256
RUN_COMM = True
RUN_COMPUTE = True

LN1G, LN1B, LN2G, LN2B, BOUT, BPROJ, BATTN, BFC = range(8)


def fori(lower, upper, body):
    lax.fori_loop(lower, upper, lambda i, c: (body(i), c)[1], 0)


def kernel(n, tok, lens, ln1g, ln1b, b_attn, b_out, ln2g, ln2b, b_fc, b_proj, w_attn, w_out, w_fc, w_proj,
           out, kc, vc, g_vec, g_attn, g_main, g_proj,
           x, h, inner, wa, wm, wp, vecs, vp, vp16, gv,
           recv, d2d, sent, load_sem, io_sem, cache_sem):
    layers = w_attn.shape[0]
    prompts, seq, width = tok.shape
    head = kc.shape[-1]
    heads = width // head
    ff = b_fc.shape[1] * n
    tokens = prompts * seq
    qkv = width + 2 * head
    per_layer = 2 + FC_PARTS + PROJ_PARTS
    chunks = 1 + layers * per_layer
    fc_cols = ff // FC_PARTS
    pr_cols = width // PROJ_PARTS

    side = math.isqrt(n // 2)
    me = lax.axis_index("dp")
    core = me % 2
    px = (me // 2) % side
    py = me // (2 * side)

    def dev(dx, dy):
        return (((py + dy + side) % side) * side + (px + dx + side) % side) * 2 + core

    sibling = me + 1 - 2 * core
    xp, xm, yp, ym = dev(1, 0), dev(-1, 0), dev(0, 1), dev(0, -1)

    def owner(dx, dy):
        return dev(-dx, -dy)

    vp[...] = jnp.zeros_like(vp)
    for k, ref in ((LN1G, ln1g), (LN1B, ln1b), (LN2G, ln2g), (LN2B, ln2b), (BOUT, b_out), (BPROJ, b_proj), (BATTN, b_attn), (BFC, b_fc)):
        wide = ref[...].astype(F32)
        for layer in range(layers):
            vp[layer * VROWS + k:layer * VROWS + k + 1, 0:ref.shape[1]] = wide[layer:layer + 1, :]
    vp16[...] = vp[...].astype(BF16)

    for p in range(prompts):
        pltpu.make_async_copy(tok.at[p], x.at[pl.ds(p * seq, seq), :], io_sem.at[p]).start()

    barrier = pltpu.get_barrier_semaphore()
    for other in (xp, xm, yp, ym, sibling):
        pl.semaphore_signal(barrier, inc=1, device_id={"dp": other})
    pl.semaphore_wait(barrier, 5)

    def layer_of(j):
        return (j - 1) // per_layer, (j - 1) % per_layer

    def by_kind(j, fn):
        layer, r = layer_of(j)

        @pl.when(j == 0)
        def _():
            fn(g_vec)

        @pl.when((j > 0) & (r == 0))
        def _():
            fn(g_attn.at[layer])

        @pl.when((j > 0) & (r >= 1) & (r < 2 + FC_PARTS))
        def _():
            fn(g_main.at[layer, r - 1])

        @pl.when((j > 0) & (r >= 2 + FC_PARTS))
        def _():
            fn(g_proj.at[layer, r - 2 - FC_PARTS])

    def own_by_kind(j, fn):
        layer, r = layer_of(j)

        @pl.when(j == 0)
        def _():
            fn(vp16, g_vec)

        @pl.when((j > 0) & (r == 0))
        def _():
            fn(w_attn.at[layer], g_attn.at[layer])

        @pl.when((j > 0) & (r == 1))
        def _():
            fn(w_out.at[layer], g_main.at[layer, 0])

        @pl.when((j > 0) & (r >= 2) & (r < 2 + FC_PARTS))
        def _():
            c = r - 2
            fn(w_fc.at[layer, :, pl.ds(pl.multiple_of(c * fc_cols, fc_cols), fc_cols)], g_main.at[layer, r - 1])

        @pl.when((j > 0) & (r >= 2 + FC_PARTS))
        def _():
            c = r - 2 - FC_PARTS
            fn(w_proj.at[layer, :, pl.ds(pl.multiple_of(c * pr_cols, pr_cols), pr_cols)], g_proj.at[layer, c])

    def wait_shards(view, count, sem):
        part = view.at[pl.ds(0, count)]
        pltpu.make_async_copy(part, part, sem).wait()

    def push(src, dst, j, sem, device):
        pltpu.make_async_remote_copy(src_ref=src, dst_ref=dst, send_sem=sent.at[j], recv_sem=sem, device_id={"dp": device}).start()

    def relay(view, j, event, moves):
        rows, cols = view.shape[1], view.shape[2]
        half_r, half_c = rows // 2, cols // 2
        whole_r, whole_c = pl.ds(0, rows), pl.ds(0, cols)
        top, bottom = pl.ds(0, half_r), pl.ds(half_r, half_r)
        left, right = pl.ds(0, half_c), pl.ds(half_c, half_c)
        cut = dict(top=(top, whole_c), bottom=(bottom, whole_c), left=(whole_r, left), right=(whole_r, right),
                   a=(top, left), b=(top, right), c=(bottom, left), d=(bottom, right))
        for (dx, dy), name, target in moves:
            block = view.at[owner(dx, dy)].at[cut[name]]
            push(block, block, j, recv.at[event, j], target)

    def hand_over(view, j, offsets):
        for dx, dy in offsets:
            block = view.at[owner(dx, dy)]
            push(block, block, j, d2d.at[j], sibling)

    def event0(j):
        def go(src, view):
            for target in (xp, xm, yp, ym):
                push(src, view.at[me], j, recv.at[0, j], target)
            push(src, view.at[me], j, d2d.at[j], sibling)
        own_by_kind(j, go)

    def event1(j):
        def go(view):
            wait_shards(view, 4, recv.at[0, j])
            relay(view, j, 1, (
                ((1, 0), "left", xp), ((-1, 0), "right", xm), ((0, 1), "left", yp), ((0, -1), "right", ym),
                ((0, 1), "bottom", xp), ((0, 1), "bottom", xm), ((1, 0), "top", yp), ((1, 0), "top", ym),
                ((0, -1), "bottom", xp), ((0, -1), "bottom", xm), ((-1, 0), "top", yp), ((-1, 0), "top", ym)))
            hand_over(view, j, ((1, 0), (-1, 0), (0, 1), (0, -1)))
        by_kind(j, go)

    def event2(j):
        def go(view):
            wait_shards(view, 6, recv.at[1, j])
            relay(view, j, 2, (
                ((0, 2), "bottom", xp), ((0, 2), "bottom", xm), ((2, 0), "top", yp), ((2, 0), "top", ym),
                ((1, 1), "c", xp), ((-1, 1), "d", xm), ((1, 1), "a", yp), ((1, -1), "b", ym),
                ((1, -1), "c", xp), ((-1, -1), "d", xm), ((-1, 1), "a", yp), ((-1, -1), "b", ym)))
            hand_over(view, j, ((2, 0), (0, 2), (1, 1), (1, -1), (-1, 1), (-1, -1)))
        by_kind(j, go)

    def event3(j):
        def go(view):
            wait_shards(view, 4, recv.at[2, j])
            relay(view, j, 3, (((1, 2), "c", xp), ((-1, 2), "d", xm), ((2, 1), "a", yp), ((2, -1), "b", ym)))
            hand_over(view, j, ((2, 1), (2, -1), (1, 2), (-1, 2)))
        by_kind(j, go)

    def event4(j):
        def go(view):
            wait_shards(view, 1, recv.at[3, j])
            hand_over(view, j, ((2, 2),))
        by_kind(j, go)

    def pump(t):
        for event, shift in ((event4, -1), (event3, 0), (event2, 1), (event1, 2), (event0, 3)):
            j = t + shift
            pl.when((j >= 0) & (j < chunks))(functools.partial(event, j))

    def load(view, own, slot, j):
        rows = view.shape[1]
        if RUN_COMM:
            wait_shards(view, n // 2, d2d.at[j])

        def one(d):
            place = slot.at[pl.ds(pl.multiple_of(d * rows, rows), rows), :]

            @pl.when(d != me)
            def _():
                pltpu.make_async_copy(view.at[d], place, load_sem).start()

            @pl.when(d == me)
            def _():
                pltpu.make_async_copy(own, place, load_sem).start()

        fori(0, n, one)
        pltpu.make_async_copy(slot, slot, load_sem).wait()

    def spread_vectors():
        load(g_vec, vp16, gv, 0)
        rows = gv.shape[0]
        for layer in range(layers):
            for k, part, total in ((LN1G, width // n, width), (LN1B, width // n, width), (LN2G, width // n, width),
                                   (LN2B, width // n, width), (BOUT, width // n, width), (BPROJ, width // n, width),
                                   (BATTN, qkv // n, qkv), (BFC, ff // n, ff)):
                dd = lax.broadcasted_iota(jnp.int32, (n, rows), 0)
                rr = lax.broadcasted_iota(jnp.int32, (n, rows), 1)
                pick = jnp.where(rr == dd * (2 * VROWS) + (layer * VROWS + k), 1.0, 0.0).astype(BF16)
                piece = jnp.dot(pick, gv[...], preferred_element_type=F32).astype(BF16)
                block = total if total <= qkv else width
                for start in range(0, total, block):
                    pos = lax.broadcasted_iota(jnp.int32, (1, block), 1).astype(F32) + float(start)
                    whose = jnp.floor((pos + 0.5) * (1.0 / part))
                    lane = pos - whose * float(part)
                    cc = lax.broadcasted_iota(jnp.int32, (VCOLS, block), 0).astype(F32)
                    place = jnp.where(cc == lane, 1.0, 0.0).astype(BF16)
                    wide = jnp.dot(piece, place, preferred_element_type=F32)
                    di = lax.broadcasted_iota(jnp.int32, (n, block), 0).astype(F32)
                    row = jnp.sum(jnp.where(di == whose, wide, 0.0), axis=0, keepdims=True)
                    vecs[layer, k:k + 1, start:start + block] = row

    def layer_norm(layer, gain_row, shift_row):
        tile = 16

        def one(m):
            rows = pl.ds(pl.multiple_of(m * tile, tile), tile)
            wide = x[rows, :].astype(F32)
            mean = jnp.mean(wide, axis=-1, keepdims=True)
            centred = wide - mean
            variance = jnp.mean(centred * centred, axis=-1, keepdims=True)
            normed = centred * lax.rsqrt(variance + EPS)
            gain = vecs[layer, gain_row:gain_row + 1, 0:width]
            shift = vecs[layer, shift_row:shift_row + 1, 0:width]
            h[rows, :] = (normed * gain + shift).astype(BF16)

        fori(0, tokens // tile, one)

    m_tile = seq

    def stage_qkv(layer):
        load(g_attn.at[layer], w_attn.at[layer], wa, 1 + layer * per_layer)
        layer_norm(layer, LN1G, LN1B)
        n_tile = 2 * head

        def one(i):
            cols = pl.ds(pl.multiple_of(i * n_tile, n_tile), n_tile)
            bias = vecs[layer, BATTN:BATTN + 1, cols]
            for m in range(tokens // m_tile):
                rows = slice(m * m_tile, (m + 1) * m_tile)
                acc = jnp.dot(h[rows, :], wa[:, cols], preferred_element_type=F32)
                inner[rows, cols] = (acc + bias).astype(BF16)

        fori(0, qkv // n_tile, one)
        for p in range(prompts):
            rows = pl.ds(p * seq, seq)
            pltpu.make_async_copy(inner.at[rows, pl.ds(width, head)], kc.at[p, layer], cache_sem.at[2 * p]).start()
            pltpu.make_async_copy(inner.at[rows, pl.ds(width + head, head)], vc.at[p, layer], cache_sem.at[2 * p + 1]).start()

    def wait_caches(layer):
        for p in range(prompts):
            rows = pl.ds(p * seq, seq)
            pltpu.make_async_copy(inner.at[rows, pl.ds(width, head)], kc.at[p, layer], cache_sem.at[2 * p]).wait()
            pltpu.make_async_copy(inner.at[rows, pl.ds(width + head, head)], vc.at[p, layer], cache_sem.at[2 * p + 1]).wait()

    q_tile = 128
    scale = head ** -0.5

    def attention(p):
        length = lens[p]
        unroll = 2

        def one(i):
            for u in range(unroll):
                cols = pl.ds(pl.multiple_of((i * unroll + u) * head, head), head)
                for b in range(seq // q_tile):
                    keys = (b + 1) * q_tile
                    rows = slice(p * seq + b * q_tile, p * seq + (b + 1) * q_tile)
                    query = inner[rows, cols]
                    kk = inner[p * seq:p * seq + keys, width:width + head]
                    vv = inner[p * seq:p * seq + keys, width + head:width + 2 * head]
                    score = lax.dot_general(query, kk, (((1,), (1,)), ((), ())), preferred_element_type=F32) * scale
                    ki = lax.broadcasted_iota(jnp.int32, (q_tile, keys), 1)
                    qi = lax.broadcasted_iota(jnp.int32, (q_tile, keys), 0) + b * q_tile
                    score = jnp.where((ki <= qi) & (ki < length), score, -1e30)
                    peak = jnp.max(score, axis=-1, keepdims=True)
                    e = jnp.exp(score - peak)
                    prob = (e / jnp.sum(e, axis=-1, keepdims=True)).astype(BF16)
                    mixed = jnp.dot(prob, vv, preferred_element_type=F32)
                    h[rows, cols] = mixed.astype(BF16)

        fori(0, heads // unroll, one)

    def stage_out(layer):
        load(g_main.at[layer, 0], w_out.at[layer], wm, 2 + layer * per_layer)
        n_tile = min(512, width)

        def one(i):
            cols = pl.ds(pl.multiple_of(i * n_tile, n_tile), n_tile)
            bias = vecs[layer, BOUT:BOUT + 1, cols]
            for m in range(tokens // m_tile):
                rows = slice(m * m_tile, (m + 1) * m_tile)
                acc = jnp.dot(h[rows, :], wm[:, cols], preferred_element_type=F32)
                x[rows, cols] = (x[rows, cols].astype(F32) + (acc + bias)).astype(BF16)

        fori(0, width // n_tile, one)
        layer_norm(layer, LN2G, LN2B)

    def stage_fc(layer, c):
        base = c * fc_cols
        load(g_main.at[layer, 1 + c], w_fc.at[layer, :, pl.ds(pl.multiple_of(base, fc_cols), fc_cols)], wm,
             3 + c + layer * per_layer)
        n_tile = min(512, fc_cols)

        def one(i):
            cols = pl.ds(pl.multiple_of(i * n_tile, n_tile), n_tile)
            far = pl.ds(pl.multiple_of(base + i * n_tile, n_tile), n_tile)
            bias = vecs[layer, BFC:BFC + 1, far]
            for m in range(tokens // m_tile):
                rows = slice(m * m_tile, (m + 1) * m_tile)
                acc = jnp.dot(h[rows, :], wm[:, cols], preferred_element_type=F32) + bias
                inner[rows, far] = jax.nn.gelu(acc, approximate=True).astype(BF16)

        fori(0, fc_cols // n_tile, one)

    def stage_proj(layer, c):
        base = c * pr_cols
        cols = pl.ds(pl.multiple_of(base, pr_cols), pr_cols)
        load(g_proj.at[layer, c], w_proj.at[layer, :, cols], wp, 3 + FC_PARTS + c + layer * per_layer)
        bias = vecs[layer, BPROJ:BPROJ + 1, cols]

        def one(m):
            rows = pl.ds(pl.multiple_of(m * m_tile, m_tile), m_tile)
            acc = jnp.dot(inner[rows, :], wp[...], preferred_element_type=F32)
            x[rows, cols] = (x[rows, cols].astype(F32) + (acc + bias)).astype(BF16)

        fori(0, tokens // m_tile, one)

    def compute(t):
        layer, r = (t - 2) // per_layer, (t - 2) % per_layer
        live = (t >= 2) & (t < 2 + layers * per_layer)

        @pl.when(t == 1)
        def _():
            spread_vectors()
            for p in range(prompts):
                pltpu.make_async_copy(tok.at[p], x.at[pl.ds(p * seq, seq), :], io_sem.at[p]).wait()

        @pl.when(live & (r == 0))
        def _():
            stage_qkv(layer)

        @pl.when(live & (r == 1))
        def _():
            for p in range(prompts - 1):
                attention(p)

        @pl.when(live & (r == 2))
        def _():
            attention(prompts - 1)
            wait_caches(layer)
            stage_out(layer)

        first_fc = 3

        @pl.when(live & (r >= first_fc) & (r < first_fc + FC_PARTS))
        def _():
            stage_fc(layer, r - first_fc)

        first_proj = first_fc + FC_PARTS
        for_proj = r - first_proj

        @pl.when(live & (r >= first_proj))
        def _():
            lo = jnp.where(for_proj == 2, PROJ_PARTS - 1, for_proj)
            hi = jnp.where(for_proj == 0, 1, jnp.where(for_proj == 1, PROJ_PARTS - 1, PROJ_PARTS))
            fori(lo, hi, lambda c: stage_proj(layer, c))

    def slot_step(i):
        t = i - 3
        if RUN_COMM:
            pump(t)
        if RUN_COMPUTE:
            compute(t)

    fori(0, chunks + 4, slot_step)

    for p in range(prompts):
        pltpu.make_async_copy(x.at[pl.ds(p * seq, seq), :], out.at[p], io_sem.at[p]).start()
    if not RUN_COMPUTE and RUN_COMM:
        fori(0, chunks, lambda j: by_kind(j, lambda view: wait_shards(view, n // 2, d2d.at[j])))
    if RUN_COMM:
        fori(0, chunks, lambda j: by_kind(j, lambda view: wait_shards(view, n - 1, sent.at[j])))
    for p in range(prompts):
        pltpu.make_async_copy(x.at[pl.ds(p * seq, seq), :], out.at[p], io_sem.at[p]).wait()


def solution(mesh):
    n = mesh.shape["dp"]
    tok_spec = P(('part', 'dp'), None, None)
    len_spec = P(('part', 'dp'))
    cache_spec = P(('part', 'dp'), None, None, None)
    vec_spec = P(None, 'dp')
    mat_spec = P(None, 'dp', None)

    def local(tokens, lengths, ln1_gain, ln1_bias, w_attn, b_attn, w_out, b_out, ln2_gain, ln2_bias, w_fc, b_fc, w_proj, b_proj):
        layers = w_attn.shape[0]
        prompts, seq, width = tokens.shape
        qkv = w_attn.shape[2]
        head = (qkv - width) // 2
        ff = w_fc.shape[2]
        rows = prompts * seq
        per_layer = 2 + FC_PARTS + PROJ_PARTS
        chunks = 1 + layers * per_layer
        r_in, r_ff = width // n, ff // n
        assert ff // FC_PARTS == width and layers * VROWS <= 2 * VROWS
        anywhere = pl.BlockSpec(memory_space=pl.ANY)
        vmem = pl.BlockSpec(memory_space=pltpu.VMEM)
        smem = pl.BlockSpec(memory_space=pltpu.SMEM)
        sds = jax.ShapeDtypeStruct
        cache = sds((prompts, layers, seq, head), BF16)
        results = pl.pallas_call(
            functools.partial(kernel, n),
            out_shape=(sds(tokens.shape, BF16), cache, cache,
                       sds((n, 2 * VROWS, VCOLS), BF16),
                       sds((layers, n, r_in, qkv), BF16),
                       sds((layers, 1 + FC_PARTS, n, r_in, width), BF16),
                       sds((layers, PROJ_PARTS, n, r_ff, width // PROJ_PARTS), BF16)),
            in_specs=[anywhere, smem] + [vmem] * 8 + [anywhere] * 4,
            out_specs=(anywhere,) * 7,
            scratch_shapes=[
                pltpu.VMEM((rows, width), BF16),
                pltpu.VMEM((rows, width), BF16),
                pltpu.VMEM((rows, ff), BF16),
                pltpu.VMEM((width, qkv), BF16),
                pltpu.VMEM((width, width), BF16),
                pltpu.VMEM((ff, width // PROJ_PARTS), BF16),
                pltpu.VMEM((layers, 8, ff), F32),
                pltpu.VMEM((2 * VROWS, VCOLS), F32),
                pltpu.VMEM((2 * VROWS, VCOLS), BF16),
                pltpu.VMEM((n * 2 * VROWS, VCOLS), BF16),
                pltpu.SemaphoreType.DMA((4, chunks)),
                pltpu.SemaphoreType.DMA((chunks,)),
                pltpu.SemaphoreType.DMA((chunks,)),
                pltpu.SemaphoreType.DMA,
                pltpu.SemaphoreType.DMA((prompts,)),
                pltpu.SemaphoreType.DMA((2 * prompts,)),
            ],
            compiler_params=pltpu.CompilerParams(collective_id=0, has_side_effects=True, vmem_limit_bytes=67043328),
            name="gather_layers",
        )(tokens, lengths, ln1_gain, ln1_bias, b_attn, b_out, ln2_gain, ln2_bias, b_fc, b_proj, w_attn, w_out, w_fc, w_proj)
        return results[0], results[1], results[2]

    return jax.shard_map(local, mesh=mesh,
                         in_specs=(tok_spec, len_spec, vec_spec, vec_spec, mat_spec, vec_spec, mat_spec, vec_spec, vec_spec, vec_spec, mat_spec, vec_spec, mat_spec, vec_spec),
                         out_specs=(tok_spec, cache_spec, cache_spec), check_vma=False)
```

time: 720 us -> 613 us (0.85); the launches traced: 712 us -> 612 us
  Pallas kernels: 0 us -> 605 us
  matrix products: 324 us -> 0 us
  waiting for transfers between devices: 145 us -> 0 us
  blocking collectives: 111 us -> 0 us
  other arithmetic: 81.1 us -> 0 us
  local copies, waits for them, and re-layouts: 35.6 us -> 6.98 us
  between operations: 15.1 us -> 0.66 us
    pallas_call x0 -> x1, Pallas kernels: none -> 605 us  [local(): pl.pallas_call(functools.partial(kernel, n), out_shape=(sds(tokens.shape,...]
    dot_general x12 -> x0, matrix products: 324 us -> none  [the longest x8 275 us: dense(): jnp.einsum('bsd,de->bse', activation, weight, preferred_element_type=jnp....]
    all_gather x8 -> x0, waiting for transfers between devices: 142 us -> none  [local(): lax.all_gather(weight_stack[layer], 'dp', axis=0, tiled=True)]
    sub x2 -> x0, other arithmetic: 64.3 us -> none  [attention(): attn_prob = jax.nn.softmax(scores, axis=-1).astype(jnp.bfloat16)]
    all_gather x2 -> x0, blocking collectives: 59.2 us -> none  [local(): lax.all_gather(weight_stack[layer], 'dp', axis=0, tiled=True)]
    unnamed x1 -> x0, blocking collectives: 51.4 us -> none
    unnamed x93 -> x7, local copies, waits for them, and re-layouts: 25.2 us -> 6.98 us
    reduce_sum x5 -> x0, other arithmetic: 10.8 us -> none  [the longest x4 7.79 us: layer_norm(): variance = jnp.mean(centred * centred, axis=-1, keepdims=True)]
  transfers between devices with their start and end apart: 8 -> 0, of which waited for: 3 -> 0; matrix products, arithmetic and copies ran while one was open for 53% -> 0% of each run, Pallas kernels for 0% -> 0%
where the time goes in v1:
time: 613 us; the launch traced here: 612 us
  Pallas kernels  605 us (99%)
  local copies, waits for them, and re-layouts  6.98 us (1%)
    pallas_call x1, Pallas kernels, local(): pl.pallas_call(functools.partial(kernel, n), out_shape=(sds(tokens.shape,...  605 us

profile of v1, /device:TPU:97, one launch (start us, length us, event | category | flops | bytes accessed | tf_op | source)
XLA Modules:
  0.0 612.4 jit_solution(13927523563673919936)
XLA Ops:
  0.6 604.7 %gather_layers.1 = (bf16[3,384,2048]{2,1,0:T(8,128)(2,1)}, bf16[3,2,384,128]{3,2,1,0:T(8,128)(2,1)}, bf16[3,2,384,128]{3,2,1,0:T(8,128)(2,1)}, bf16[32,32,256]{2...) custom-call(bf16[3,384,2048]{2,1,0:T(8,128)(2,1)} %tok.1, ...), custom_call_target="tpu_custom_call" | custom-call | tf_op jit(solution)/shard_map/gather_layers/pallas_call | solution.py:431
  605.4 0.0 copy-start.1
  605.4 0.0 copy-start
  605.4 5.3 copy.20
  610.7 0.0 copy-done.1
  610.7 0.8 copy.21
  611.5 0.0 copy-done
  611.5 0.8 copy.22
Async XLA Ops:
  605.4 5.4 copy-start.1
  605.4 6.2 %copy-start = (bf16[3,2,384,128]{3,2,1,0:T(8,128)(2,1)S(1)}, bf16[3,2,384,128]{3,2,1,0:T(8,128)(2,1)}, u32[]{:S(2)}) copy-start(bf16[3,2,384,128]{3,2,1,0:T(8,128)(2,1)} %get-tuple-element.14) | copy-start | bytes 1769476

commit v2 on v1

--- a/solution.py
+++ b/solution.py
@@ -15,6 +15,8 @@
 PROJ_PARTS = 4
 VROWS = 16
 VCOLS = 256
+SLOTS = 3
+LATE = 3
 RUN_COMM = True
 RUN_COMPUTE = True
 
@@ -27,8 +29,8 @@
 
 def kernel(n, tok, lens, ln1g, ln1b, b_attn, b_out, ln2g, ln2b, b_fc, b_proj, w_attn, w_out, w_fc, w_proj,
            out, kc, vc, g_vec, g_attn, g_main, g_proj,
-           x, h, inner, wa, wm, wp, vecs, vp, vp16, gv,
-           recv, d2d, sent, load_sem, io_sem, cache_sem):
+           x, h, inner, ws, vecs, vp, vp16, gv,
+           recv, d2d, sent, load_sem, vec_sem, io_sem, cache_sem):
     layers = w_attn.shape[0]
     prompts, seq, width = tok.shape
     head = kc.shape[-1]
@@ -93,12 +95,13 @@
         def _():
             fn(g_proj.at[layer, r - 2 - FC_PARTS])
 
-    def own_by_kind(j, fn):
+    def own_by_kind(j, fn, vectors=True):
         layer, r = layer_of(j)
 
-        @pl.when(j == 0)
-        def _():
-            fn(vp16, g_vec)
+        if vectors:
+            @pl.when(j == 0)
+            def _():
+                fn(vp16, g_vec)
 
         @pl.when((j > 0) & (r == 0))
         def _():
@@ -182,32 +185,61 @@
             hand_over(view, j, ((2, 2),))
         by_kind(j, go)
 
+    late = chunks - LATE
+
+    def when_chunk(event, j):
+        pl.when((j >= 0) & (j < chunks))(lambda: event(j))
+
+    def early(t, far, near):
+        return jnp.where(t + far < late, t + far, jnp.where(t + near >= late, t + near, chunks))
+
     def pump(t):
-        for event, shift in ((event4, -1), (event3, 0), (event2, 1), (event1, 2), (event0, 3)):
-            j = t + shift
-            pl.when((j >= 0) & (j < chunks))(functools.partial(event, j))
-
-    def load(view, own, slot, j):
-        rows = view.shape[1]
+        when_chunk(event3, t)
+        when_chunk(event2, t + 1)
+        when_chunk(event1, early(t, 3, 2))
+        when_chunk(event0, early(t, 5, 3))
+
+    fold = ff // width
+    band_rows = width * n // ff
+
+    def fetch(view, own, put, sem, j):
         if RUN_COMM:
             wait_shards(view, n // 2, d2d.at[j])
 
         def one(d):
-            place = slot.at[pl.ds(pl.multiple_of(d * rows, rows), rows), :]
-
             @pl.when(d != me)
             def _():
-                pltpu.make_async_copy(view.at[d], place, load_sem).start()
+                pltpu.make_async_copy(view.at[d], put(d), sem).start()
 
             @pl.when(d == me)
             def _():
-                pltpu.make_async_copy(own, place, load_sem).start()
+                pltpu.make_async_copy(own, put(d), sem).start()
 
         fori(0, n, one)
-        pltpu.make_async_copy(slot, slot, load_sem).wait()
+
+    def fetch_chunk(j):
+        slot, sem = ws.at[j % SLOTS], load_sem.at[j % SLOTS]
+
+        def go(own, view):
+            rows, cols = view.shape[1], view.shape[2]
+            if rows * n == width:
+                def put(d):
+                    return slot.at[pl.ds(pl.multiple_of(d * rows, rows), rows), pl.ds(0, cols)]
+            else:
+                def put(d):
+                    return slot.at[pl.ds(pl.multiple_of((d % band_rows) * rows, rows), rows),
+                                   pl.ds(pl.multiple_of((d // band_rows) * cols, cols), cols)]
+            fetch(view, own, put, sem, j)
+
+        own_by_kind(j, go, vectors=False)
+
+    def wait_chunk(j, cols):
+        part = ws.at[j % SLOTS].at[:, pl.ds(0, cols)]
+        pltpu.make_async_copy(part, part, load_sem.at[j % SLOTS]).wait()
 
     def spread_vectors():
-        load(g_vec, vp16, gv, 0)
+        fetch(g_vec, vp16, lambda d: gv.at[pl.ds(pl.multiple_of(d * 2 * VROWS, 2 * VROWS), 2 * VROWS), :], vec_sem, 0)
+        pltpu.make_async_copy(gv, gv, vec_sem).wait()
         rows = gv.shape[0]
         for layer in range(layers):
             for k, part, total in ((LN1G, width // n, width), (LN1B, width // n, width), (LN2G, width // n, width),
@@ -230,41 +262,52 @@
                     vecs[layer, k:k + 1, start:start + block] = row
 
     def layer_norm(layer, gain_row, shift_row):
-        tile = 16
-
-        def one(m):
-            rows = pl.ds(pl.multiple_of(m * tile, tile), tile)
-            wide = x[rows, :].astype(F32)
-            mean = jnp.mean(wide, axis=-1, keepdims=True)
-            centred = wide - mean
-            variance = jnp.mean(centred * centred, axis=-1, keepdims=True)
-            normed = centred * lax.rsqrt(variance + EPS)
-            gain = vecs[layer, gain_row:gain_row + 1, 0:width]
-            shift = vecs[layer, shift_row:shift_row + 1, 0:width]
-            h[rows, :] = (normed * gain + shift).astype(BF16)
-
-        fori(0, tokens // tile, one)
+        tile, unroll = 16, 4
+
+        def one(i):
+            for u in range(unroll):
+                rows = pl.ds(pl.multiple_of((i * unroll + u) * tile, tile), tile)
+                wide = x[rows, :].astype(F32)
+                mean = jnp.mean(wide, axis=-1, keepdims=True)
+                centred = wide - mean
+                variance = jnp.mean(centred * centred, axis=-1, keepdims=True)
+                normed = centred * lax.rsqrt(variance + EPS)
+                gain = vecs[layer, gain_row:gain_row + 1, 0:width]
+                shift = vecs[layer, shift_row:shift_row + 1, 0:width]
+                h[rows, :] = (normed * gain + shift).astype(BF16)
+
+        fori(0, tokens // (tile * unroll), one)
 
     m_tile = seq
 
-    def stage_qkv(layer):
-        load(g_attn.at[layer], w_attn.at[layer], wa, 1 + layer * per_layer)
-        layer_norm(layer, LN1G, LN1B)
+    def stage_qkv(layer, half):
+        j = 1 + layer * per_layer
         n_tile = 2 * head
+        tiles = qkv // n_tile
+
+        @pl.when(half == 0)
+        def _():
+            @pl.when(layer > 0)
+            def _():
+                layer_norm(layer, LN1G, LN1B)
+            wait_chunk(j, qkv)
 
         def one(i):
             cols = pl.ds(pl.multiple_of(i * n_tile, n_tile), n_tile)
             bias = vecs[layer, BATTN:BATTN + 1, cols]
             for m in range(tokens // m_tile):
                 rows = slice(m * m_tile, (m + 1) * m_tile)
-                acc = jnp.dot(h[rows, :], wa[:, cols], preferred_element_type=F32)
+                acc = jnp.dot(h[rows, :], ws[j % SLOTS, :, cols], preferred_element_type=F32)
                 inner[rows, cols] = (acc + bias).astype(BF16)
 
-        fori(0, qkv // n_tile, one)
-        for p in range(prompts):
-            rows = pl.ds(p * seq, seq)
-            pltpu.make_async_copy(inner.at[rows, pl.ds(width, head)], kc.at[p, layer], cache_sem.at[2 * p]).start()
-            pltpu.make_async_copy(inner.at[rows, pl.ds(width + head, head)], vc.at[p, layer], cache_sem.at[2 * p + 1]).start()
+        fori(half * (tiles // 2), tiles // 2 + half * (tiles - tiles // 2), one)
+
+        @pl.when(half == 1)
+        def _():
+            for p in range(prompts):
+                rows = pl.ds(p * seq, seq)
+                pltpu.make_async_copy(inner.at[rows, pl.ds(width, head)], kc.at[p, layer], cache_sem.at[2 * p]).start()
+                pltpu.make_async_copy(inner.at[rows, pl.ds(width + head, head)], vc.at[p, layer], cache_sem.at[2 * p + 1]).start()
 
     def wait_caches(layer):
         for p in range(prompts):
@@ -273,35 +316,41 @@
             pltpu.make_async_copy(inner.at[rows, pl.ds(width + head, head)], vc.at[p, layer], cache_sem.at[2 * p + 1]).wait()
 
     q_tile = 128
-    scale = head ** -0.5
+    group = 4
+    to_log2 = head ** -0.5 * math.log2(math.e)
+    masked = -1e30 * head ** 0.5
 
     def attention(p):
         length = lens[p]
-        unroll = 2
+        start = p * seq
 
         def one(i):
-            for u in range(unroll):
-                cols = pl.ds(pl.multiple_of((i * unroll + u) * head, head), head)
-                for b in range(seq // q_tile):
-                    keys = (b + 1) * q_tile
-                    rows = slice(p * seq + b * q_tile, p * seq + (b + 1) * q_tile)
-                    query = inner[rows, cols]
-                    kk = inner[p * seq:p * seq + keys, width:width + head]
-                    vv = inner[p * seq:p * seq + keys, width + head:width + 2 * head]
-                    score = lax.dot_general(query, kk, (((1,), (1,)), ((), ())), preferred_element_type=F32) * scale
-                    ki = lax.broadcasted_iota(jnp.int32, (q_tile, keys), 1)
-                    qi = lax.broadcasted_iota(jnp.int32, (q_tile, keys), 0) + b * q_tile
-                    score = jnp.where((ki <= qi) & (ki < length), score, -1e30)
+            for b in range(seq // q_tile):
+                keys = (b + 1) * q_tile
+                rows = slice(start + b * q_tile, start + (b + 1) * q_tile)
+                cols = [pl.ds(pl.multiple_of((i * group + u) * head, head), head) for u in range(group)]
+                query = jnp.concatenate([inner[rows, c] for c in cols], axis=0)
+                kk = inner[start:start + keys, width:width + head]
+                vv = inner[start:start + keys, width + head:width + 2 * head]
+                scores = lax.dot_general(query, kk, (((1,), (1,)), ((), ())), preferred_element_type=F32)
+                ki = lax.broadcasted_iota(jnp.int32, (q_tile, keys), 1)
+                qi = lax.broadcasted_iota(jnp.int32, (q_tile, keys), 0) + b * q_tile
+                allowed = (ki <= qi) & (ki < length)
+                probs = []
+                for u in range(group):
+                    score = jnp.where(allowed, scores[u * q_tile:(u + 1) * q_tile, :], masked)
                     peak = jnp.max(score, axis=-1, keepdims=True)
-                    e = jnp.exp(score - peak)
-                    prob = (e / jnp.sum(e, axis=-1, keepdims=True)).astype(BF16)
-                    mixed = jnp.dot(prob, vv, preferred_element_type=F32)
-                    h[rows, cols] = mixed.astype(BF16)
-
-        fori(0, heads // unroll, one)
+                    e = jnp.exp2((score - peak) * to_log2)
+                    probs.append((e * (1.0 / jnp.sum(e, axis=-1, keepdims=True))).astype(BF16))
+                mixed = jnp.dot(jnp.concatenate(probs, axis=0), vv, preferred_element_type=F32).astype(BF16)
+                for u in range(group):
+                    h[rows, cols[u]] = mixed[u * q_tile:(u + 1) * q_tile, :]
+
+        fori(0, heads // group, one)
 
     def stage_out(layer):
-        load(g_main.at[layer, 0], w_out.at[layer], wm, 2 + layer * per_layer)
+        j = 2 + layer * per_layer
+        wait_chunk(j, width)
         n_tile = min(512, width)
 
         def one(i):
@@ -309,16 +358,16 @@
             bias = vecs[layer, BOUT:BOUT + 1, cols]
             for m in range(tokens // m_tile):
                 rows = slice(m * m_tile, (m + 1) * m_tile)
-                acc = jnp.dot(h[rows, :], wm[:, cols], preferred_element_type=F32)
+                acc = jnp.dot(h[rows, :], ws[j % SLOTS, :, cols], preferred_element_type=F32)
                 x[rows, cols] = (x[rows, cols].astype(F32) + (acc + bias)).astype(BF16)
 
         fori(0, width // n_tile, one)
-        layer_norm(layer, LN2G, LN2B)
-
-    def stage_fc(layer, c):
+
+    def stage_fc(layer, unit):
+        c, part = unit // 2, unit % 2
         base = c * fc_cols
-        load(g_main.at[layer, 1 + c], w_fc.at[layer, :, pl.ds(pl.multiple_of(base, fc_cols), fc_cols)], wm,
-             3 + c + layer * per_layer)
+        j = 3 + c + layer * per_layer
+        pl.when(part == 0)(lambda: wait_chunk(j, fc_cols))
         n_tile = min(512, fc_cols)
 
         def one(i):
@@ -327,81 +376,104 @@
             bias = vecs[layer, BFC:BFC + 1, far]
             for m in range(tokens // m_tile):
                 rows = slice(m * m_tile, (m + 1) * m_tile)
-                acc = jnp.dot(h[rows, :], wm[:, cols], preferred_element_type=F32) + bias
+                acc = jnp.dot(h[rows, :], ws[j % SLOTS, :, cols], preferred_element_type=F32) + bias
                 inner[rows, far] = jax.nn.gelu(acc, approximate=True).astype(BF16)
 
-        fori(0, fc_cols // n_tile, one)
-
-    def stage_proj(layer, c):
+        tiles = fc_cols // n_tile
+        fori(part * (tiles // 2), tiles // 2 + part * (tiles - tiles // 2), one)
+
+    def stage_proj(layer, c, half):
         base = c * pr_cols
         cols = pl.ds(pl.multiple_of(base, pr_cols), pr_cols)
-        load(g_proj.at[layer, c], w_proj.at[layer, :, cols], wp, 3 + FC_PARTS + c + layer * per_layer)
+        j = 3 + FC_PARTS + c + layer * per_layer
+        pl.when(half == 0)(lambda: wait_chunk(j, width))
         bias = vecs[layer, BPROJ:BPROJ + 1, cols]
 
         def one(m):
             rows = pl.ds(pl.multiple_of(m * m_tile, m_tile), m_tile)
-            acc = jnp.dot(inner[rows, :], wp[...], preferred_element_type=F32)
-            x[rows, cols] = (x[rows, cols].astype(F32) + (acc + bias)).astype(BF16)
-
-        fori(0, tokens // m_tile, one)
-
-    def compute(t):
+            acc = bias
+            for q in range(fold):
+                acc = acc + jnp.dot(inner[rows, q * width:(q + 1) * width], ws[j % SLOTS, :, q * pr_cols:(q + 1) * pr_cols],
+                                    preferred_element_type=F32)
+            x[rows, cols] = (x[rows, cols].astype(F32) + acc).astype(BF16)
+
+        tiles = tokens // m_tile
+        cut = tiles - tiles // 2
+        fori(half * cut, cut + half * (tiles - cut), one)
+
+        @pl.when((layer == layers - 1) & (half == 1))
+        def _():
+            for p in range(prompts):
+                pltpu.make_async_copy(x.at[pl.ds(p * seq, seq), cols], out.at[p, :, cols], io_sem.at[0]).start()
+
+    first_fc, first_proj = 3, 2 + FC_PARTS
+
+    def compute(t, half):
         layer, r = (t - 2) // per_layer, (t - 2) % per_layer
         live = (t >= 2) & (t < 2 + layers * per_layer)
 
-        @pl.when(t == 1)
+        @pl.when((t == 1) & (half == 0))
         def _():
             spread_vectors()
             for p in range(prompts):
                 pltpu.make_async_copy(tok.at[p], x.at[pl.ds(p * seq, seq), :], io_sem.at[p]).wait()
 
+        @pl.when((t == 1) & (half == 1))
+        def _():
+            layer_norm(0, LN1G, LN1B)
+
         @pl.when(live & (r == 0))
         def _():
-            stage_qkv(layer)
-
-        @pl.when(live & (r == 1))
-        def _():
-            for p in range(prompts - 1):
-                attention(p)
-
-        @pl.when(live & (r == 2))
-        def _():
-            attention(prompts - 1)
+            stage_qkv(layer, half)
+
+        for p in range(prompts):
+            pl.when(live & (r == 1) & (half == (p == prompts - 1)))(functools.partial(attention, p))
+
+        @pl.when(live & (r == 2) & (half == 0))
+        def _():
             wait_caches(layer)
             stage_out(layer)
 
-        first_fc = 3
-
-        @pl.when(live & (r >= first_fc) & (r < first_fc + FC_PARTS))
-        def _():
-            stage_fc(layer, r - first_fc)
-
-        first_proj = first_fc + FC_PARTS
-        for_proj = r - first_proj
+        @pl.when(live & (r == 2) & (half == 1))
+        def _():
+            layer_norm(layer, LN2G, LN2B)
+
+        @pl.when(live & (r >= first_fc) & (r < first_proj))
+        def _():
+            lo = 3 * (r - first_fc) + 2 * half
+            hi = jnp.minimum(lo + 2 - half, 2 * FC_PARTS)
+            fori(lo, hi, lambda unit: stage_fc(layer, unit))
 
         @pl.when(live & (r >= first_proj))
         def _():
-            lo = jnp.where(for_proj == 2, PROJ_PARTS - 1, for_proj)
-            hi = jnp.where(for_proj == 0, 1, jnp.where(for_proj == 1, PROJ_PARTS - 1, PROJ_PARTS))
-            fori(lo, hi, lambda c: stage_proj(layer, c))
+            stage_proj(layer, r - first_proj, half)
 
     def slot_step(i):
-        t = i - 3
+        t, half = i // 2 - 5, i % 2
         if RUN_COMM:
-            pump(t)
+            pl.when(half == 0)(lambda: pump(t))
+            pl.when(half == 1)(lambda: when_chunk(event4, t))
         if RUN_COMPUTE:
-            compute(t)
-
-    fori(0, chunks + 4, slot_step)
-
-    for p in range(prompts):
-        pltpu.make_async_copy(x.at[pl.ds(p * seq, seq), :], out.at[p], io_sem.at[p]).start()
+            pl.when((half == 1) & (t >= 1) & (t < chunks))(lambda: fetch_chunk(t))
+            compute(t, half)
+
+    if not RUN_COMPUTE:
+        for p in range(prompts):
+            pltpu.make_async_copy(tok.at[p], x.at[pl.ds(p * seq, seq), :], io_sem.at[p]).wait()
+            pltpu.make_async_copy(x.at[pl.ds(p * seq, seq), :], out.at[p], io_sem.at[0]).start()
+    fori(0, 2 * (chunks + 6), slot_step)
+
     if not RUN_COMPUTE and RUN_COMM:
         fori(0, chunks, lambda j: by_kind(j, lambda view: wait_shards(view, n // 2, d2d.at[j])))
     if RUN_COMM:
         fori(0, chunks, lambda j: by_kind(j, lambda view: wait_shards(view, n - 1, sent.at[j])))
-    for p in range(prompts):
-        pltpu.make_async_copy(x.at[pl.ds(p * seq, seq), :], out.at[p], io_sem.at[p]).wait()
+    pltpu.make_async_copy(x, x, io_sem.at[0]).wait()
+
+
+def hand_out(a, b, c, a_out, b_out, c_out):
+    a_out[...] = a[...]
+    b_out[...] = b[...]
+    c_out[...] = c[...]
 
 
 def solution(mesh):
@@ -441,9 +513,7 @@
                 pltpu.VMEM((rows, width), BF16),
                 pltpu.VMEM((rows, width), BF16),
                 pltpu.VMEM((rows, ff), BF16),
-                pltpu.VMEM((width, qkv), BF16),
-                pltpu.VMEM((width, width), BF16),
-                pltpu.VMEM((ff, width // PROJ_PARTS), BF16),
+                pltpu.VMEM((SLOTS, width, qkv), BF16),
                 pltpu.VMEM((layers, 8, ff), F32),
                 pltpu.VMEM((2 * VROWS, VCOLS), F32),
                 pltpu.VMEM((2 * VROWS, VCOLS), BF16),
@@ -451,6 +521,7 @@
                 pltpu.SemaphoreType.DMA((4, chunks)),
                 pltpu.SemaphoreType.DMA((chunks,)),
                 pltpu.SemaphoreType.DMA((chunks,)),
+                pltpu.SemaphoreType.DMA((SLOTS,)),
                 pltpu.SemaphoreType.DMA,
                 pltpu.SemaphoreType.DMA((prompts,)),
                 pltpu.SemaphoreType.DMA((2 * prompts,)),
@@ -458,7 +529,17 @@
             compiler_params=pltpu.CompilerParams(collective_id=0, has_side_effects=True, vmem_limit_bytes=67043328),
             name="gather_layers",
         )(tokens, lengths, ln1_gain, ln1_bias, b_attn, b_out, ln2_gain, ln2_bias, b_fc, b_proj, w_attn, w_out, w_fc, w_proj)
-        return results[0], results[1], results[2]
+        block = lambda shape: pl.BlockSpec((1,) + shape[1:], lambda i: (i,) + (0,) * (len(shape) - 1))
+        shapes = (tokens.shape, cache.shape, cache.shape)
+        return pl.pallas_call(
+            hand_out,
+            grid=(prompts,),
+            out_shape=(sds(tokens.shape, BF16), cache, cache),
+            in_specs=[block(shape) for shape in shapes],
+            out_specs=tuple(block(shape) for shape in shapes),
+            compiler_params=pltpu.CompilerParams(dimension_semantics=("arbitrary",)),
+            name="hand_out",
+        )(*results[:3])
 
     return jax.shard_map(local, mesh=mesh,
                          in_specs=(tok_spec, len_spec, vec_spec, vec_spec, mat_spec, vec_spec, mat_spec, vec_spec, vec_spec, vec_spec, mat_spec, vec_spec, mat_spec, vec_spec),

time: 613 us -> 484 us (0.79)
  Pallas kernels: 605 us -> 483 us
  local copies, waits for them, and re-layouts: 6.98 us -> 0 us
    pallas_call x1, Pallas kernels: 605 us -> 477 us  [local(): pl.pallas_call(functools.partial(kernel, n), out_shape=(sds(tokens.shape,...]
    unnamed x7 -> x0, local copies, waits for them, and re-layouts: 6.98 us -> none
where the time goes in v2:
time: 484 us
  Pallas kernels  483 us (100%)
    pallas_call x1, Pallas kernels, local(): pl.pallas_call(functools.partial(kernel, n), out_shape=(sds(tokens.shape,...  477 us

profile of v2, /device:TPU:97, one launch (start us, length us, event | category | flops | bytes accessed | tf_op | source)
XLA Modules:
  0.0 483.6 jit_solution(13620147670768028405)
XLA Ops:
  0.6 476.9 %gather_layers.1 = (bf16[3,384,2048]{2,1,0:T(8,128)(2,1)}, bf16[3,2,384,128]{3,2,1,0:T(8,128)(2,1)}, bf16[3,2,384,128]{3,2,1,0:T(8,128)(2,1)}, bf16[32,32,256]{2...) custom-call(bf16[3,384,2048]{2,1,0:T(8,128)(2,1)} %tok.1, ...), custom_call_target="tpu_custom_call" | custom-call | tf_op jit(solution)/shard_map/gather_layers/pallas_call | solution.py:503
  477.5 6.1 %hand_out.1 = (bf16[3,384,2048]{2,1,0:T(8,128)(2,1)}, bf16[3,2,384,128]{3,2,1,0:T(8,128)(2,1)}, bf16[3,2,384,128]{3,2,1,0:T(8,128)(2,1)}) custom-call(bf16[3,384,2048]{2,1,0:T(8,128)(2,1)} %get-tuple-element.6.a, bf16[3,2,384,128]{3,2,1,0:T(8,128)(2,1)} %get-tuple-element.7.b, bf16[3,2,384,128]{3,2,1,0:T(8,128)(2,1)} %get-tuple-element.8.c), custom_call_target="tpu_custom_call" | custom-call | tf_op jit(solution)/shard_map/hand_out/pallas_call | solution.py:534

commit v3 on v2

--- a/solution.py
+++ b/solution.py
@@ -13,10 +13,11 @@
 BF16 = jnp.bfloat16
 FC_PARTS = 4
 PROJ_PARTS = 4
+LAST_WIDE = 3
 VROWS = 16
 VCOLS = 256
 SLOTS = 3
-LATE = 3
+LATE = 2
 RUN_COMM = True
 RUN_COMPUTE = True
 
@@ -39,9 +40,10 @@
     tokens = prompts * seq
     qkv = width + 2 * head
     per_layer = 2 + FC_PARTS + PROJ_PARTS
-    chunks = 1 + layers * per_layer
+    chunks = 1 + layers * per_layer + (PROJ_PARTS - LAST_WIDE)
     fc_cols = ff // FC_PARTS
     pr_cols = width // PROJ_PARTS
+    half_cols = pr_cols // 2
 
     side = math.isqrt(n // 2)
     me = lax.axis_index("dp")
@@ -74,7 +76,15 @@
     pl.semaphore_wait(barrier, 5)
 
     def layer_of(j):
-        return (j - 1) // per_layer, (j - 1) % per_layer
+        layer = jnp.minimum((j - 1) // per_layer, layers - 1)
+        return layer, j - 1 - layer * per_layer
+
+    def is_narrow(layer, r):
+        return (layer == layers - 1) & (r >= 2 + FC_PARTS + LAST_WIDE)
+
+    def narrow_part(r):
+        q = r - (2 + FC_PARTS + LAST_WIDE)
+        return LAST_WIDE + q // 2, pl.ds(pl.multiple_of((q % 2) * half_cols, half_cols), half_cols)
 
     def by_kind(j, fn):
         layer, r = layer_of(j)
@@ -91,9 +101,16 @@
         def _():
             fn(g_main.at[layer, r - 1])
 
-        @pl.when((j > 0) & (r >= 2 + FC_PARTS))
+        narrow = is_narrow(layer, r)
+
+        @pl.when((j > 0) & (r >= 2 + FC_PARTS) & jnp.logical_not(narrow))
         def _():
             fn(g_proj.at[layer, r - 2 - FC_PARTS])
+
+        @pl.when((j > 0) & narrow)
+        def _():
+            c, cols = narrow_part(r)
+            fn(g_proj.at[layer, c].at[:, :, cols])
 
     def own_by_kind(j, fn, vectors=True):
         layer, r = layer_of(j)
@@ -116,7 +133,15 @@
             c = r - 2
             fn(w_fc.at[layer, :, pl.ds(pl.multiple_of(c * fc_cols, fc_cols), fc_cols)], g_main.at[layer, r - 1])
 
-        @pl.when((j > 0) & (r >= 2 + FC_PARTS))
+        narrow = is_narrow(layer, r)
+
+        @pl.when((j > 0) & narrow)
+        def _():
+            c, cols = narrow_part(r)
+            far = pl.ds(pl.multiple_of(c * pr_cols + cols.start, half_cols), half_cols)
+            fn(w_proj.at[layer, :, far], g_proj.at[layer, c].at[:, :, cols])
+
+        @pl.when((j > 0) & (r >= 2 + FC_PARTS) & jnp.logical_not(narrow))
         def _():
             c = r - 2 - FC_PARTS
             fn(w_proj.at[layer, :, pl.ds(pl.multiple_of(c * pr_cols, pr_cols), pr_cols)], g_proj.at[layer, c])
@@ -406,11 +431,28 @@
             for p in range(prompts):
                 pltpu.make_async_copy(x.at[pl.ds(p * seq, seq), cols], out.at[p, :, cols], io_sem.at[0]).start()
 
+    def stage_proj_narrow(layer, r):
+        c, cols = narrow_part(r)
+        far = pl.ds(pl.multiple_of(c * pr_cols + cols.start, half_cols), half_cols)
+        j = 1 + layer * per_layer + r
+        wait_chunk(j, fold * half_cols)
+        bias = vecs[layer, BPROJ:BPROJ + 1, far]
+        for m in range(tokens // m_tile):
+            rows = slice(m * m_tile, (m + 1) * m_tile)
+            acc = bias
+            for q in range(fold):
+                acc = acc + jnp.dot(inner[rows, q * width:(q + 1) * width], ws[j % SLOTS, :, q * half_cols:(q + 1) * half_cols],
+                                    preferred_element_type=F32)
+            x[rows, far] = (x[rows, far].astype(F32) + acc).astype(BF16)
+        for p in range(prompts):
+            pltpu.make_async_copy(x.at[pl.ds(p * seq, seq), far], out.at[p, :, far], io_sem.at[0]).start()
+
     first_fc, first_proj = 3, 2 + FC_PARTS
 
     def compute(t, half):
-        layer, r = (t - 2) // per_layer, (t - 2) % per_layer
-        live = (t >= 2) & (t < 2 + layers * per_layer)
+        layer, r = layer_of(t - 1)
+        live = (t >= 2) & (t < 1 + chunks)
+        narrow = is_narrow(layer, r)
 
         @pl.when((t == 1) & (half == 0))
         def _():
@@ -444,9 +486,13 @@
             hi = jnp.minimum(lo + 2 - half, 2 * FC_PARTS)
             fori(lo, hi, lambda unit: stage_fc(layer, unit))
 
-        @pl.when(live & (r >= first_proj))
+        @pl.when(live & (r >= first_proj) & jnp.logical_not(narrow))
         def _():
             stage_proj(layer, r - first_proj, half)
+
+        @pl.when(live & narrow & (half == 0))
+        def _():
+            stage_proj_narrow(layer, r)
 
     def slot_step(i):
         t, half = i // 2 - 5, i % 2
@@ -492,7 +538,7 @@
         ff = w_fc.shape[2]
         rows = prompts * seq
         per_layer = 2 + FC_PARTS + PROJ_PARTS
-        chunks = 1 + layers * per_layer
+        chunks = 1 + layers * per_layer + (PROJ_PARTS - LAST_WIDE)
         r_in, r_ff = width // n, ff // n
         assert ff // FC_PARTS == width and layers * VROWS <= 2 * VROWS
         anywhere = pl.BlockSpec(memory_space=pl.ANY)

time: 484 us -> 483 us (level)
  no operation moved by 1% of the time
where the time goes in v3:
time: 483 us; the launch traced here: 482 us
  Pallas kernels  482 us (100%)
    pallas_call x1, Pallas kernels, local(): pl.pallas_call(functools.partial(kernel, n), out_shape=(sds(tokens.shape,...  476 us

profile of v3, /device:TPU:97, one launch (start us, length us, event | category | flops | bytes accessed | tf_op | source)
XLA Modules:
  0.0 482.3 jit_solution(16982801605678002502)
XLA Ops:
  0.6 475.6 %gather_layers.1 = (bf16[3,384,2048]{2,1,0:T(8,128)(2,1)}, bf16[3,2,384,128]{3,2,1,0:T(8,128)(2,1)}, bf16[3,2,384,128]{3,2,1,0:T(8,128)(2,1)}, bf16[32,32,256]{2...) custom-call(bf16[3,384,2048]{2,1,0:T(8,128)(2,1)} %tok.1, ...), custom_call_target="tpu_custom_call" | custom-call | tf_op jit(solution)/shard_map/gather_layers/pallas_call | solution.py:549
  476.2 6.1 %hand_out.1 = (bf16[3,384,2048]{2,1,0:T(8,128)(2,1)}, bf16[3,2,384,128]{3,2,1,0:T(8,128)(2,1)}, bf16[3,2,384,128]{3,2,1,0:T(8,128)(2,1)}) custom-call(bf16[3,384,2048]{2,1,0:T(8,128)(2,1)} %get-tuple-element.6.a, bf16[3,2,384,128]{3,2,1,0:T(8,128)(2,1)} %get-tuple-element.7.b, bf16[3,2,384,128]{3,2,1,0:T(8,128)(2,1)} %get-tuple-element.8.c), custom_call_target="tpu_custom_call" | custom-call | tf_op jit(solution)/shard_map/hand_out/pallas_call | solution.py:580
